TPU v7x, 32 devices: a 4x4x1 block of a 4x4x8 slice. The times are simulated.
32 devices in a mesh: batch: 1 (over z), cy: 4 (over y), cx: 8 (over x, core).
Axes of the slice: x: 4, y: 4, z: 1, core: 2. Of those that a mesh axis runs over, the one named last changes fastest.
The devices are a block of a 4x4x8 slice.
Arguments:
- q_seq: bfloat16 [4096, 32, 64], P(('batch', 'cx', 'cy'))
- k_seq: bfloat16 [4096, 8, 64], P(('batch', 'cx', 'cy'))
- v_seq: bfloat16 [4096, 8, 64], P(('batch', 'cx', 'cy'))
Outputs:
- output: bfloat16 [4096, 32, 64], P(('batch', 'cx', 'cy'))
All inputs are finite; a program needn't handle non-finite values.
Results may differ from a plain program's by a relative error of at most 0.00508428.
Values are sent between devices in bfloat16 or wider.
A program may use at most 768 MiB of HBM per device.

v0:
```python
import math
import jax
import jax.numpy as jnp
from jax import lax
from jax.sharding import PartitionSpec as P


def block_update(running, q_grouped, k_blk, v_blk):
    row_max, row_sum, out_acc = running
    score_scale = 1.0 / math.sqrt(q_grouped.shape[-1])
    scores = jnp.einsum("qkgd,skd->kgqs", q_grouped, k_blk, preferred_element_type=jnp.float32) * score_scale
    new_max = jnp.maximum(row_max, jnp.max(scores, axis=-1))
    rescale = jnp.exp(row_max - new_max)
    prob_blk = jnp.exp(scores - new_max[..., None])
    row_sum = row_sum * rescale + jnp.sum(prob_blk, axis=-1)
    weighted = jnp.einsum("kgqs,skd->kgqd", prob_blk.astype(jnp.bfloat16), v_blk, preferred_element_type=jnp.float32)
    out_acc = out_acc * rescale[..., None] + weighted
    return new_max, row_sum, out_acc


def start_state(q_grouped):
    tokens, num_kv, groups, head_dim = q_grouped.shape
    row_max = jnp.full((num_kv, groups, tokens), -jnp.inf, jnp.float32)
    row_sum = jnp.zeros((num_kv, groups, tokens), jnp.float32)
    out_acc = jnp.zeros((num_kv, groups, tokens, head_dim), jnp.float32)
    return row_max, row_sum, out_acc


def finish(running, tokens, num_heads, head_dim):
    row_max, row_sum, out_acc = running
    result = out_acc / row_sum[..., None]
    return jnp.transpose(result, (2, 0, 1, 3)).reshape(tokens, num_heads, head_dim).astype(jnp.bfloat16)


def solution(mesh):
    size_x = mesh.shape["cx"]
    size_y = mesh.shape["cy"]
    seq_spec = P(("batch", "cx", "cy"), None, None)
    perm_x = [(dev_idx, (dev_idx + 1) % size_x) for dev_idx in range(size_x)]
    perm_y = [(dev_idx, (dev_idx + 1) % size_y) for dev_idx in range(size_y)]

    def local_attention(q_local, k_local, v_local):
        tokens, num_heads, head_dim = q_local.shape
        num_kv = k_local.shape[1]
        q_grouped = q_local.reshape(tokens, num_kv, num_heads // num_kv, head_dim)

        def step_x(step_idx, loop_state):
            running, k_blk, v_blk = loop_state
            running = block_update(running, q_grouped, k_blk, v_blk)
            k_blk = lax.ppermute(k_blk, "cx", perm_x)
            v_blk = lax.ppermute(v_blk, "cx", perm_x)
            return running, k_blk, v_blk

        def sweep_x(loop_state):
            running, k_blk, v_blk = lax.fori_loop(0, size_x - 1, step_x, loop_state)
            return block_update(running, q_grouped, k_blk, v_blk), k_blk, v_blk

        def step_y(step_idx, loop_state):
            running, k_blk, v_blk = sweep_x(loop_state)
            k_blk = lax.ppermute(k_blk, "cy", perm_y)
            v_blk = lax.ppermute(v_blk, "cy", perm_y)
            return running, k_blk, v_blk

        loop_state = lax.fori_loop(0, size_y - 1, step_y, (start_state(q_grouped), k_local, v_local))
        running = sweep_x(loop_state)[0]
        return finish(running, tokens, num_heads, head_dim)

    return jax.shard_map(local_attention, mesh=mesh, in_specs=(seq_spec, seq_spec, seq_spec), out_specs=seq_spec, check_vma=False)
```

profile of v0, /device:TPU:97, one launch (start us, length us, event | category | flops | bytes accessed | tf_op | source)
XLA Modules:
  0.0 225.8 jit_solution(16720889363816526294)
XLA Ops:
  1.8 170.0 %while.58 = (s32[]{:T(128)}, f32[8,4,128]{2,1,0:T(4,128)S(1)}, f32[8,4,128]{2,1,0:T(4,128)S(1)}, f32[8,4,128,64]{2,3,1,0:T(8,128)S(1)}, bf16[128,8,64]{0,2,1:T(8...) while((s32[]{:T(128)}, f32[8,4,128]{2,1,0:T(4,128)S(1)}, ...), condition=%wide.region_7.0_spmd.clone, body=%wide.region_0.0_spmd.clone.sunk | while | flops 278159360 | bytes 26247624 | solution.py:64
  2.9 45.5 %while.59 = (s32[]{:T(128)}, f32[8,4,128]{2,1,0:T(4,128)S(1)}, f32[8,4,128]{2,1,0:T(4,128)S(1)}, f32[8,4,128,64]{2,3,1,0:T(8,128)S(1)}, bf16[128,8,64]{0,2,1:T(8...) while((s32[]{:T(128)}, f32[8,4,128]{2,1,0:T(4,128)S(1)}, ...), condition=%wide.region_4.0_spmd, body=%wide.region_1.0_spmd.sunk | while | flops 138944512 | bytes 11010213 | solution.py:55
  2.9 2.7 %collective-permute-start.2 = (bf16[128,8,64]{0,2,1:T(8,128)(2,1)S(1)}, bf16[128,8,64]{0,2,1:T(8,128)(2,1)S(1)}, u32[]{:S(2)}, u32[]{:S(2)}) collective-permute-start(bf16[128,8,64]{0,2,1:T(8,128)(2,1)S(1)} %copy.30), channel_id=1, source_target_pairs={{0,1},{1,2},{2,3},{3,4},{4,5},{5,6},{6,7},{7,0},{8,9},{9,10},{10,1... | collective-permute-start | bytes 393224 | tf_op jit(solution)/shard_map/while/body/eval_jaxpr/while/body/eval_jaxpr/ppermute | solution.py:50
  8.9 2.5 %collective-permute-start.2 = (bf16[128,8,64]{0,2,1:T(8,128)(2,1)S(1)}, bf16[128,8,64]{0,2,1:T(8,128)(2,1)S(1)}, u32[]{:S(2)}, u32[]{:S(2)}) collective-permute-start(bf16[128,8,64]{0,2,1:T(8,128)(2,1)S(1)} %copy.30), channel_id=1, source_target_pairs={{0,1},{1,2},{2,3},{3,4},{4,5},{5,6},{6,7},{7,0},{8,9},{9,10},{10,1... | collective-permute-start | bytes 393224 | tf_op jit(solution)/shard_map/while/body/eval_jaxpr/while/body/eval_jaxpr/ppermute | solution.py:50
  14.7 2.5 %collective-permute-start.2 = (bf16[128,8,64]{0,2,1:T(8,128)(2,1)S(1)}, bf16[128,8,64]{0,2,1:T(8,128)(2,1)S(1)}, u32[]{:S(2)}, u32[]{:S(2)}) collective-permute-start(bf16[128,8,64]{0,2,1:T(8,128)(2,1)S(1)} %copy.30), channel_id=1, source_target_pairs={{0,1},{1,2},{2,3},{3,4},{4,5},{5,6},{6,7},{7,0},{8,9},{9,10},{10,1... | collective-permute-start | bytes 393224 | tf_op jit(solution)/shard_map/while/body/eval_jaxpr/while/body/eval_jaxpr/ppermute | solution.py:50
  20.6 2.5 %collective-permute-start.2 = (bf16[128,8,64]{0,2,1:T(8,128)(2,1)S(1)}, bf16[128,8,64]{0,2,1:T(8,128)(2,1)S(1)}, u32[]{:S(2)}, u32[]{:S(2)}) collective-permute-start(bf16[128,8,64]{0,2,1:T(8,128)(2,1)S(1)} %copy.30), channel_id=1, source_target_pairs={{0,1},{1,2},{2,3},{3,4},{4,5},{5,6},{6,7},{7,0},{8,9},{9,10},{10,1... | collective-permute-start | bytes 393224 | tf_op jit(solution)/shard_map/while/body/eval_jaxpr/while/body/eval_jaxpr/ppermute | solution.py:50
  25.0 2.0 collective-permute-done.2
  27.2 1.8 collective-permute-start.2
  30.8 3.3 %collective-permute-done.2 = bf16[128,8,64]{0,2,1:T(8,128)(2,1)S(1)} collective-permute-done((bf16[128,8,64]{0,2,1:T(8,128)(2,1)S(1)}, bf16[128,8,64]{0,2,1:T(8,128)(2,1)S(1)}, u32[]{:S(2)}, u32[]{:S(2)}) %collective-permute-start.2) | collective-permute-done | bytes 131104 | tf_op jit(solution)/shard_map/while/body/eval_jaxpr/while/body/eval_jaxpr/ppermute | solution.py:50
  36.7 4.5 %collective-permute-done.2 = bf16[128,8,64]{0,2,1:T(8,128)(2,1)S(1)} collective-permute-done((bf16[128,8,64]{0,2,1:T(8,128)(2,1)S(1)}, bf16[128,8,64]{0,2,1:T(8,128)(2,1)S(1)}, u32[]{:S(2)}, u32[]{:S(2)}) %collective-permute-start.2) | collective-permute-done | bytes 131104 | tf_op jit(solution)/shard_map/while/body/eval_jaxpr/while/body/eval_jaxpr/ppermute | solution.py:50
  43.2 5.0 %collective-permute-done.2 = bf16[128,8,64]{0,2,1:T(8,128)(2,1)S(1)} collective-permute-done((bf16[128,8,64]{0,2,1:T(8,128)(2,1)S(1)}, bf16[128,8,64]{0,2,1:T(8,128)(2,1)S(1)}, u32[]{:S(2)}, u32[]{:S(2)}) %collective-permute-start.2) | collective-permute-done | bytes 131104 | tf_op jit(solution)/shard_map/while/body/eval_jaxpr/while/body/eval_jaxpr/ppermute | solution.py:50
  49.6 1.8 collective-permute-start.5
  54.5 1.4 collective-permute-done.5
  57.0 50.3 %while.59 = (s32[]{:T(128)}, f32[8,4,128]{2,1,0:T(4,128)S(1)}, f32[8,4,128]{2,1,0:T(4,128)S(1)}, f32[8,4,128,64]{2,3,1,0:T(8,128)S(1)}, bf16[128,8,64]{0,2,1:T(8...) while((s32[]{:T(128)}, f32[8,4,128]{2,1,0:T(4,128)S(1)}, ...), condition=%wide.region_4.0_spmd, body=%wide.region_1.0_spmd.sunk | while | flops 138944512 | bytes 11010213 | solution.py:55
  59.8 4.9 %collective-permute-done.2 = bf16[128,8,64]{0,2,1:T(8,128)(2,1)S(1)} collective-permute-done((bf16[128,8,64]{0,2,1:T(8,128)(2,1)S(1)}, bf16[128,8,64]{0,2,1:T(8,128)(2,1)S(1)}, u32[]{:S(2)}, u32[]{:S(2)}) %collective-permute-start.2) | collective-permute-done | bytes 131104 | tf_op jit(solution)/shard_map/while/body/eval_jaxpr/while/body/eval_jaxpr/ppermute | solution.py:50
  66.8 5.0 %collective-permute-done.2 = bf16[128,8,64]{0,2,1:T(8,128)(2,1)S(1)} collective-permute-done((bf16[128,8,64]{0,2,1:T(8,128)(2,1)S(1)}, bf16[128,8,64]{0,2,1:T(8,128)(2,1)S(1)}, u32[]{:S(2)}, u32[]{:S(2)}) %collective-permute-start.2) | collective-permute-done | bytes 131104 | tf_op jit(solution)/shard_map/while/body/eval_jaxpr/while/body/eval_jaxpr/ppermute | solution.py:50
  73.9 5.0 %collective-permute-done.2 = bf16[128,8,64]{0,2,1:T(8,128)(2,1)S(1)} collective-permute-done((bf16[128,8,64]{0,2,1:T(8,128)(2,1)S(1)}, bf16[128,8,64]{0,2,1:T(8,128)(2,1)S(1)}, u32[]{:S(2)}, u32[]{:S(2)}) %collective-permute-start.2) | collective-permute-done | bytes 131104 | tf_op jit(solution)/shard_map/while/body/eval_jaxpr/while/body/eval_jaxpr/ppermute | solution.py:50
  80.9 5.0 %collective-permute-done.2 = bf16[128,8,64]{0,2,1:T(8,128)(2,1)S(1)} collective-permute-done((bf16[128,8,64]{0,2,1:T(8,128)(2,1)S(1)}, bf16[128,8,64]{0,2,1:T(8,128)(2,1)S(1)}, u32[]{:S(2)}, u32[]{:S(2)}) %collective-permute-start.2) | collective-permute-done | bytes 131104 | tf_op jit(solution)/shard_map/while/body/eval_jaxpr/while/body/eval_jaxpr/ppermute | solution.py:50
  88.0 5.0 %collective-permute-done.2 = bf16[128,8,64]{0,2,1:T(8,128)(2,1)S(1)} collective-permute-done((bf16[128,8,64]{0,2,1:T(8,128)(2,1)S(1)}, bf16[128,8,64]{0,2,1:T(8,128)(2,1)S(1)}, u32[]{:S(2)}, u32[]{:S(2)}) %collective-permute-start.2) | collective-permute-done | bytes 131104 | tf_op jit(solution)/shard_map/while/body/eval_jaxpr/while/body/eval_jaxpr/ppermute | solution.py:50
  95.1 5.0 %collective-permute-done.2 = bf16[128,8,64]{0,2,1:T(8,128)(2,1)S(1)} collective-permute-done((bf16[128,8,64]{0,2,1:T(8,128)(2,1)S(1)}, bf16[128,8,64]{0,2,1:T(8,128)(2,1)S(1)}, u32[]{:S(2)}, u32[]{:S(2)}) %collective-permute-start.2) | collective-permute-done | bytes 131104 | tf_op jit(solution)/shard_map/while/body/eval_jaxpr/while/body/eval_jaxpr/ppermute | solution.py:50
  102.1 5.0 %collective-permute-done.2 = bf16[128,8,64]{0,2,1:T(8,128)(2,1)S(1)} collective-permute-done((bf16[128,8,64]{0,2,1:T(8,128)(2,1)S(1)}, bf16[128,8,64]{0,2,1:T(8,128)(2,1)S(1)}, u32[]{:S(2)}, u32[]{:S(2)}) %collective-permute-start.2) | collective-permute-done | bytes 131104 | tf_op jit(solution)/shard_map/while/body/eval_jaxpr/while/body/eval_jaxpr/ppermute | solution.py:50
  107.3 1.5 collective-permute-start.5
  110.5 2.1 collective-permute-done.4
  114.8 50.6 %while.59 = (s32[]{:T(128)}, f32[8,4,128]{2,1,0:T(4,128)S(1)}, f32[8,4,128]{2,1,0:T(4,128)S(1)}, f32[8,4,128,64]{2,3,1,0:T(8,128)S(1)}, bf16[128,8,64]{0,2,1:T(8...) while((s32[]{:T(128)}, f32[8,4,128]{2,1,0:T(4,128)S(1)}, ...), condition=%wide.region_4.0_spmd, body=%wide.region_1.0_spmd.sunk | while | flops 138944512 | bytes 11010213 | solution.py:55
  116.7 6.1 %collective-permute-done.2 = bf16[128,8,64]{0,2,1:T(8,128)(2,1)S(1)} collective-permute-done((bf16[128,8,64]{0,2,1:T(8,128)(2,1)S(1)}, bf16[128,8,64]{0,2,1:T(8,128)(2,1)S(1)}, u32[]{:S(2)}, u32[]{:S(2)}) %collective-permute-start.2) | collective-permute-done | bytes 131104 | tf_op jit(solution)/shard_map/while/body/eval_jaxpr/while/body/eval_jaxpr/ppermute | solution.py:50
  124.9 5.0 %collective-permute-done.2 = bf16[128,8,64]{0,2,1:T(8,128)(2,1)S(1)} collective-permute-done((bf16[128,8,64]{0,2,1:T(8,128)(2,1)S(1)}, bf16[128,8,64]{0,2,1:T(8,128)(2,1)S(1)}, u32[]{:S(2)}, u32[]{:S(2)}) %collective-permute-start.2) | collective-permute-done | bytes 131104 | tf_op jit(solution)/shard_map/while/body/eval_jaxpr/while/body/eval_jaxpr/ppermute | solution.py:50
  132.0 5.0 %collective-permute-done.2 = bf16[128,8,64]{0,2,1:T(8,128)(2,1)S(1)} collective-permute-done((bf16[128,8,64]{0,2,1:T(8,128)(2,1)S(1)}, bf16[128,8,64]{0,2,1:T(8,128)(2,1)S(1)}, u32[]{:S(2)}, u32[]{:S(2)}) %collective-permute-start.2) | collective-permute-done | bytes 131104 | tf_op jit(solution)/shard_map/while/body/eval_jaxpr/while/body/eval_jaxpr/ppermute | solution.py:50
  139.0 5.0 %collective-permute-done.2 = bf16[128,8,64]{0,2,1:T(8,128)(2,1)S(1)} collective-permute-done((bf16[128,8,64]{0,2,1:T(8,128)(2,1)S(1)}, bf16[128,8,64]{0,2,1:T(8,128)(2,1)S(1)}, u32[]{:S(2)}, u32[]{:S(2)}) %collective-permute-start.2) | collective-permute-done | bytes 131104 | tf_op jit(solution)/shard_map/while/body/eval_jaxpr/while/body/eval_jaxpr/ppermute | solution.py:50
  146.1 5.0 %collective-permute-done.2 = bf16[128,8,64]{0,2,1:T(8,128)(2,1)S(1)} collective-permute-done((bf16[128,8,64]{0,2,1:T(8,128)(2,1)S(1)}, bf16[128,8,64]{0,2,1:T(8,128)(2,1)S(1)}, u32[]{:S(2)}, u32[]{:S(2)}) %collective-permute-start.2) | collective-permute-done | bytes 131104 | tf_op jit(solution)/shard_map/while/body/eval_jaxpr/while/body/eval_jaxpr/ppermute | solution.py:50
  153.2 5.0 %collective-permute-done.2 = bf16[128,8,64]{0,2,1:T(8,128)(2,1)S(1)} collective-permute-done((bf16[128,8,64]{0,2,1:T(8,128)(2,1)S(1)}, bf16[128,8,64]{0,2,1:T(8,128)(2,1)S(1)}, u32[]{:S(2)}, u32[]{:S(2)}) %collective-permute-start.2) | collective-permute-done | bytes 131104 | tf_op jit(solution)/shard_map/while/body/eval_jaxpr/while/body/eval_jaxpr/ppermute | solution.py:50
  160.2 5.0 %collective-permute-done.2 = bf16[128,8,64]{0,2,1:T(8,128)(2,1)S(1)} collective-permute-done((bf16[128,8,64]{0,2,1:T(8,128)(2,1)S(1)}, bf16[128,8,64]{0,2,1:T(8,128)(2,1)S(1)}, u32[]{:S(2)}, u32[]{:S(2)}) %collective-permute-start.2) | collective-permute-done | bytes 131104 | tf_op jit(solution)/shard_map/while/body/eval_jaxpr/while/body/eval_jaxpr/ppermute | solution.py:50
  167.4 3.3 %collective-permute-done.4 = bf16[128,8,64]{0,2,1:T(8,128)(2,1)S(1)} collective-permute-done((bf16[128,8,64]{0,2,1:T(8,128)(2,1)S(1)}, bf16[128,8,64]{0,2,1:T(8,128)(2,1)S(1)}, u32[]{:S(2)}, u32[]{:S(2)}) %collective-permute-start.4) | collective-permute-done | bytes 131104 | tf_op jit(solution)/shard_map/while/body/eval_jaxpr/ppermute | solution.py:60
  171.8 50.6 %while.56 = (s32[]{:T(128)}, f32[8,4,128]{2,1,0:T(4,128)S(1)}, f32[8,4,128]{2,1,0:T(4,128)S(1)}, f32[8,4,128,64]{2,3,1,0:T(8,128)S(1)}, bf16[128,8,64]{0,2,1:T(8...) while((s32[]{:T(128)}, f32[8,4,128]{2,1,0:T(4,128)S(1)}, ...), condition=%wide.region_11.0_spmd, body=%wide.region_8.0_spmd.sunk | while | flops 138944512 | bytes 11010213 | solution.py:55
  172.0 1.5 bitcast_reduce_fusion.7
  174.8 5.1 %collective-permute-done = bf16[128,8,64]{0,2,1:T(8,128)(2,1)S(1)} collective-permute-done((bf16[128,8,64]{0,2,1:T(8,128)(2,1)S(1)}, bf16[128,8,64]{0,2,1:T(8,128)(2,1)S(1)}, u32[]{:S(2)}, u32[]{:S(2)}) %collective-permute-start) | collective-permute-done | bytes 131104 | tf_op jit(solution)/shard_map/while/body/eval_jaxpr/ppermute | solution.py:50
  180.2 1.5 bitcast_reduce_fusion.7
  183.0 3.9 %collective-permute-done = bf16[128,8,64]{0,2,1:T(8,128)(2,1)S(1)} collective-permute-done((bf16[128,8,64]{0,2,1:T(8,128)(2,1)S(1)}, bf16[128,8,64]{0,2,1:T(8,128)(2,1)S(1)}, u32[]{:S(2)}, u32[]{:S(2)}) %collective-permute-start) | collective-permute-done | bytes 131104 | tf_op jit(solution)/shard_map/while/body/eval_jaxpr/ppermute | solution.py:50
  187.3 1.5 bitcast_reduce_fusion.7
  190.1 3.9 %collective-permute-done = bf16[128,8,64]{0,2,1:T(8,128)(2,1)S(1)} collective-permute-done((bf16[128,8,64]{0,2,1:T(8,128)(2,1)S(1)}, bf16[128,8,64]{0,2,1:T(8,128)(2,1)S(1)}, u32[]{:S(2)}, u32[]{:S(2)}) %collective-permute-start) | collective-permute-done | bytes 131104 | tf_op jit(solution)/shard_map/while/body/eval_jaxpr/ppermute | solution.py:50
  194.4 1.5 bitcast_reduce_fusion.7
  197.1 3.9 %collective-permute-done = bf16[128,8,64]{0,2,1:T(8,128)(2,1)S(1)} collective-permute-done((bf16[128,8,64]{0,2,1:T(8,128)(2,1)S(1)}, bf16[128,8,64]{0,2,1:T(8,128)(2,1)S(1)}, u32[]{:S(2)}, u32[]{:S(2)}) %collective-permute-start) | collective-permute-done | bytes 131104 | tf_op jit(solution)/shard_map/while/body/eval_jaxpr/ppermute | solution.py:50
  201.4 1.5 bitcast_reduce_fusion.7
  204.2 3.9 %collective-permute-done = bf16[128,8,64]{0,2,1:T(8,128)(2,1)S(1)} collective-permute-done((bf16[128,8,64]{0,2,1:T(8,128)(2,1)S(1)}, bf16[128,8,64]{0,2,1:T(8,128)(2,1)S(1)}, u32[]{:S(2)}, u32[]{:S(2)}) %collective-permute-start) | collective-permute-done | bytes 131104 | tf_op jit(solution)/shard_map/while/body/eval_jaxpr/ppermute | solution.py:50
  208.5 1.5 bitcast_reduce_fusion.7
  211.3 3.9 %collective-permute-done = bf16[128,8,64]{0,2,1:T(8,128)(2,1)S(1)} collective-permute-done((bf16[128,8,64]{0,2,1:T(8,128)(2,1)S(1)}, bf16[128,8,64]{0,2,1:T(8,128)(2,1)S(1)}, u32[]{:S(2)}, u32[]{:S(2)}) %collective-permute-start) | collective-permute-done | bytes 131104 | tf_op jit(solution)/shard_map/while/body/eval_jaxpr/ppermute | solution.py:50
  215.6 1.5 bitcast_reduce_fusion.7
  218.3 3.9 %collective-permute-done = bf16[128,8,64]{0,2,1:T(8,128)(2,1)S(1)} collective-permute-done((bf16[128,8,64]{0,2,1:T(8,128)(2,1)S(1)}, bf16[128,8,64]{0,2,1:T(8,128)(2,1)S(1)}, u32[]{:S(2)}, u32[]{:S(2)}) %collective-permute-start) | collective-permute-done | bytes 131104 | tf_op jit(solution)/shard_map/while/body/eval_jaxpr/ppermute | solution.py:50
  222.5 1.5 bitcast_reduce_fusion.3
  (348 shorter events, 74.9 us)
Async XLA Ops:
  27.2 6.9 %collective-permute-start.2 = (bf16[128,8,64]{0,2,1:T(8,128)(2,1)S(1)}, bf16[128,8,64]{0,2,1:T(8,128)(2,1)S(1)}, u32[]{:S(2)}, u32[]{:S(2)}) collective-permute-start(bf16[128,8,64]{0,2,1:T(8,128)(2,1)S(1)} %copy.30), channel_id=1, source_target_pairs={{0,1},{1,2},{2,3},{3,4},{4,5},{5,6},{6,7},{7,0},{8,9},{9,10},{10,1... | collective-permute-start | bytes 393224 | tf_op jit(solution)/shard_map/while/body/eval_jaxpr/while/body/eval_jaxpr/ppermute | solution.py:50
  34.3 6.9 %collective-permute-start.2 = (bf16[128,8,64]{0,2,1:T(8,128)(2,1)S(1)}, bf16[128,8,64]{0,2,1:T(8,128)(2,1)S(1)}, u32[]{:S(2)}, u32[]{:S(2)}) collective-permute-start(bf16[128,8,64]{0,2,1:T(8,128)(2,1)S(1)} %copy.30), channel_id=1, source_target_pairs={{0,1},{1,2},{2,3},{3,4},{4,5},{5,6},{6,7},{7,0},{8,9},{9,10},{10,1... | collective-permute-start | bytes 393224 | tf_op jit(solution)/shard_map/while/body/eval_jaxpr/while/body/eval_jaxpr/ppermute | solution.py:50
  34.9 6.4 %collective-permute-start.3 = (bf16[128,8,64]{0,2,1:T(8,128)(2,1)S(1)}, bf16[128,8,64]{0,2,1:T(8,128)(2,1)S(1)}, u32[]{:S(2)}, u32[]{:S(2)}) collective-permute-start(bf16[128,8,64]{0,2,1:T(8,128)(2,1)S(1)} %copy.31), channel_id=1, source_target_pairs={{0,1},{1,2},{2,3},{3,4},{4,5},{5,6},{6,7},{7,0},{8,9},{9,10},{10,1... | collective-permute-start | bytes 393224 | tf_op jit(solution)/shard_map/while/body/eval_jaxpr/while/body/eval_jaxpr/ppermute | solution.py:51
  41.3 6.9 %collective-permute-start.2 = (bf16[128,8,64]{0,2,1:T(8,128)(2,1)S(1)}, bf16[128,8,64]{0,2,1:T(8,128)(2,1)S(1)}, u32[]{:S(2)}, u32[]{:S(2)}) collective-permute-start(bf16[128,8,64]{0,2,1:T(8,128)(2,1)S(1)} %copy.30), channel_id=1, source_target_pairs={{0,1},{1,2},{2,3},{3,4},{4,5},{5,6},{6,7},{7,0},{8,9},{9,10},{10,1... | collective-permute-start | bytes 393224 | tf_op jit(solution)/shard_map/while/body/eval_jaxpr/while/body/eval_jaxpr/ppermute | solution.py:50
  41.4 7.0 %collective-permute-start.3 = (bf16[128,8,64]{0,2,1:T(8,128)(2,1)S(1)}, bf16[128,8,64]{0,2,1:T(8,128)(2,1)S(1)}, u32[]{:S(2)}, u32[]{:S(2)}) collective-permute-start(bf16[128,8,64]{0,2,1:T(8,128)(2,1)S(1)} %copy.31), channel_id=1, source_target_pairs={{0,1},{1,2},{2,3},{3,4},{4,5},{5,6},{6,7},{7,0},{8,9},{9,10},{10,1... | collective-permute-start | bytes 393224 | tf_op jit(solution)/shard_map/while/body/eval_jaxpr/while/body/eval_jaxpr/ppermute | solution.py:51
  57.0 7.7 %collective-permute-start.2 = (bf16[128,8,64]{0,2,1:T(8,128)(2,1)S(1)}, bf16[128,8,64]{0,2,1:T(8,128)(2,1)S(1)}, u32[]{:S(2)}, u32[]{:S(2)}) collective-permute-start(bf16[128,8,64]{0,2,1:T(8,128)(2,1)S(1)} %copy.30), channel_id=1, source_target_pairs={{0,1},{1,2},{2,3},{3,4},{4,5},{5,6},{6,7},{7,0},{8,9},{9,10},{10,1... | collective-permute-start | bytes 393224 | tf_op jit(solution)/shard_map/while/body/eval_jaxpr/while/body/eval_jaxpr/ppermute | solution.py:50
  58.0 6.9 %collective-permute-start.3 = (bf16[128,8,64]{0,2,1:T(8,128)(2,1)S(1)}, bf16[128,8,64]{0,2,1:T(8,128)(2,1)S(1)}, u32[]{:S(2)}, u32[]{:S(2)}) collective-permute-start(bf16[128,8,64]{0,2,1:T(8,128)(2,1)S(1)} %copy.31), channel_id=1, source_target_pairs={{0,1},{1,2},{2,3},{3,4},{4,5},{5,6},{6,7},{7,0},{8,9},{9,10},{10,1... | collective-permute-start | bytes 393224 | tf_op jit(solution)/shard_map/while/body/eval_jaxpr/while/body/eval_jaxpr/ppermute | solution.py:51
  64.9 6.9 %collective-permute-start.2 = (bf16[128,8,64]{0,2,1:T(8,128)(2,1)S(1)}, bf16[128,8,64]{0,2,1:T(8,128)(2,1)S(1)}, u32[]{:S(2)}, u32[]{:S(2)}) collective-permute-start(bf16[128,8,64]{0,2,1:T(8,128)(2,1)S(1)} %copy.30), channel_id=1, source_target_pairs={{0,1},{1,2},{2,3},{3,4},{4,5},{5,6},{6,7},{7,0},{8,9},{9,10},{10,1... | collective-permute-start | bytes 393224 | tf_op jit(solution)/shard_map/while/body/eval_jaxpr/while/body/eval_jaxpr/ppermute | solution.py:50
  65.0 7.0 %collective-permute-start.3 = (bf16[128,8,64]{0,2,1:T(8,128)(2,1)S(1)}, bf16[128,8,64]{0,2,1:T(8,128)(2,1)S(1)}, u32[]{:S(2)}, u32[]{:S(2)}) collective-permute-start(bf16[128,8,64]{0,2,1:T(8,128)(2,1)S(1)} %copy.31), channel_id=1, source_target_pairs={{0,1},{1,2},{2,3},{3,4},{4,5},{5,6},{6,7},{7,0},{8,9},{9,10},{10,1... | collective-permute-start | bytes 393224 | tf_op jit(solution)/shard_map/while/body/eval_jaxpr/while/body/eval_jaxpr/ppermute | solution.py:51
  72.0 6.9 %collective-permute-start.2 = (bf16[128,8,64]{0,2,1:T(8,128)(2,1)S(1)}, bf16[128,8,64]{0,2,1:T(8,128)(2,1)S(1)}, u32[]{:S(2)}, u32[]{:S(2)}) collective-permute-start(bf16[128,8,64]{0,2,1:T(8,128)(2,1)S(1)} %copy.30), channel_id=1, source_target_pairs={{0,1},{1,2},{2,3},{3,4},{4,5},{5,6},{6,7},{7,0},{8,9},{9,10},{10,1... | collective-permute-start | bytes 393224 | tf_op jit(solution)/shard_map/while/body/eval_jaxpr/while/body/eval_jaxpr/ppermute | solution.py:50
  72.1 7.0 %collective-permute-start.3 = (bf16[128,8,64]{0,2,1:T(8,128)(2,1)S(1)}, bf16[128,8,64]{0,2,1:T(8,128)(2,1)S(1)}, u32[]{:S(2)}, u32[]{:S(2)}) collective-permute-start(bf16[128,8,64]{0,2,1:T(8,128)(2,1)S(1)} %copy.31), channel_id=1, source_target_pairs={{0,1},{1,2},{2,3},{3,4},{4,5},{5,6},{6,7},{7,0},{8,9},{9,10},{10,1... | collective-permute-start | bytes 393224 | tf_op jit(solution)/shard_map/while/body/eval_jaxpr/while/body/eval_jaxpr/ppermute | solution.py:51
  79.1 6.9 %collective-permute-start.2 = (bf16[128,8,64]{0,2,1:T(8,128)(2,1)S(1)}, bf16[128,8,64]{0,2,1:T(8,128)(2,1)S(1)}, u32[]{:S(2)}, u32[]{:S(2)}) collective-permute-start(bf16[128,8,64]{0,2,1:T(8,128)(2,1)S(1)} %copy.30), channel_id=1, source_target_pairs={{0,1},{1,2},{2,3},{3,4},{4,5},{5,6},{6,7},{7,0},{8,9},{9,10},{10,1... | collective-permute-start | bytes 393224 | tf_op jit(solution)/shard_map/while/body/eval_jaxpr/while/body/eval_jaxpr/ppermute | solution.py:50
  79.1 7.0 %collective-permute-start.3 = (bf16[128,8,64]{0,2,1:T(8,128)(2,1)S(1)}, bf16[128,8,64]{0,2,1:T(8,128)(2,1)S(1)}, u32[]{:S(2)}, u32[]{:S(2)}) collective-permute-start(bf16[128,8,64]{0,2,1:T(8,128)(2,1)S(1)} %copy.31), channel_id=1, source_target_pairs={{0,1},{1,2},{2,3},{3,4},{4,5},{5,6},{6,7},{7,0},{8,9},{9,10},{10,1... | collective-permute-start | bytes 393224 | tf_op jit(solution)/shard_map/while/body/eval_jaxpr/while/body/eval_jaxpr/ppermute | solution.py:51
  86.1 6.9 %collective-permute-start.2 = (bf16[128,8,64]{0,2,1:T(8,128)(2,1)S(1)}, bf16[128,8,64]{0,2,1:T(8,128)(2,1)S(1)}, u32[]{:S(2)}, u32[]{:S(2)}) collective-permute-start(bf16[128,8,64]{0,2,1:T(8,128)(2,1)S(1)} %copy.30), channel_id=1, source_target_pairs={{0,1},{1,2},{2,3},{3,4},{4,5},{5,6},{6,7},{7,0},{8,9},{9,10},{10,1... | collective-permute-start | bytes 393224 | tf_op jit(solution)/shard_map/while/body/eval_jaxpr/while/body/eval_jaxpr/ppermute | solution.py:50
  86.2 7.0 %collective-permute-start.3 = (bf16[128,8,64]{0,2,1:T(8,128)(2,1)S(1)}, bf16[128,8,64]{0,2,1:T(8,128)(2,1)S(1)}, u32[]{:S(2)}, u32[]{:S(2)}) collective-permute-start(bf16[128,8,64]{0,2,1:T(8,128)(2,1)S(1)} %copy.31), channel_id=1, source_target_pairs={{0,1},{1,2},{2,3},{3,4},{4,5},{5,6},{6,7},{7,0},{8,9},{9,10},{10,1... | collective-permute-start | bytes 393224 | tf_op jit(solution)/shard_map/while/body/eval_jaxpr/while/body/eval_jaxpr/ppermute | solution.py:51
  93.2 6.9 %collective-permute-start.2 = (bf16[128,8,64]{0,2,1:T(8,128)(2,1)S(1)}, bf16[128,8,64]{0,2,1:T(8,128)(2,1)S(1)}, u32[]{:S(2)}, u32[]{:S(2)}) collective-permute-start(bf16[128,8,64]{0,2,1:T(8,128)(2,1)S(1)} %copy.30), channel_id=1, source_target_pairs={{0,1},{1,2},{2,3},{3,4},{4,5},{5,6},{6,7},{7,0},{8,9},{9,10},{10,1... | collective-permute-start | bytes 393224 | tf_op jit(solution)/shard_map/while/body/eval_jaxpr/while/body/eval_jaxpr/ppermute | solution.py:50
  93.3 7.0 %collective-permute-start.3 = (bf16[128,8,64]{0,2,1:T(8,128)(2,1)S(1)}, bf16[128,8,64]{0,2,1:T(8,128)(2,1)S(1)}, u32[]{:S(2)}, u32[]{:S(2)}) collective-permute-start(bf16[128,8,64]{0,2,1:T(8,128)(2,1)S(1)} %copy.31), channel_id=1, source_target_pairs={{0,1},{1,2},{2,3},{3,4},{4,5},{5,6},{6,7},{7,0},{8,9},{9,10},{10,1... | collective-permute-start | bytes 393224 | tf_op jit(solution)/shard_map/while/body/eval_jaxpr/while/body/eval_jaxpr/ppermute | solution.py:51
  100.3 6.9 %collective-permute-start.2 = (bf16[128,8,64]{0,2,1:T(8,128)(2,1)S(1)}, bf16[128,8,64]{0,2,1:T(8,128)(2,1)S(1)}, u32[]{:S(2)}, u32[]{:S(2)}) collective-permute-start(bf16[128,8,64]{0,2,1:T(8,128)(2,1)S(1)} %copy.30), channel_id=1, source_target_pairs={{0,1},{1,2},{2,3},{3,4},{4,5},{5,6},{6,7},{7,0},{8,9},{9,10},{10,1... | collective-permute-start | bytes 393224 | tf_op jit(solution)/shard_map/while/body/eval_jaxpr/while/body/eval_jaxpr/ppermute | solution.py:50
  100.3 7.0 %collective-permute-start.3 = (bf16[128,8,64]{0,2,1:T(8,128)(2,1)S(1)}, bf16[128,8,64]{0,2,1:T(8,128)(2,1)S(1)}, u32[]{:S(2)}, u32[]{:S(2)}) collective-permute-start(bf16[128,8,64]{0,2,1:T(8,128)(2,1)S(1)} %copy.31), channel_id=1, source_target_pairs={{0,1},{1,2},{2,3},{3,4},{4,5},{5,6},{6,7},{7,0},{8,9},{9,10},{10,1... | collective-permute-start | bytes 393224 | tf_op jit(solution)/shard_map/while/body/eval_jaxpr/while/body/eval_jaxpr/ppermute | solution.py:51
  107.3 6.4 %collective-permute-start.5 = (bf16[128,8,64]{0,2,1:T(8,128)(2,1)S(1)}, bf16[128,8,64]{0,2,1:T(8,128)(2,1)S(1)}, u32[]{:S(2)}, u32[]{:S(2)}) collective-permute-start(bf16[128,8,64]{0,2,1:T(8,128)(2,1)S(1)} %get-tuple-element.406), channel_id=1, source_target_pairs={{0,8},{8,16},{16,24},{24,0},{1,9},{9,17},{17,25},{25,1},{2,10},{10... | collective-permute-start | bytes 393224 | tf_op jit(solution)/shard_map/while/body/eval_jaxpr/ppermute | solution.py:61
  114.8 8.0 %collective-permute-start.2 = (bf16[128,8,64]{0,2,1:T(8,128)(2,1)S(1)}, bf16[128,8,64]{0,2,1:T(8,128)(2,1)S(1)}, u32[]{:S(2)}, u32[]{:S(2)}) collective-permute-start(bf16[128,8,64]{0,2,1:T(8,128)(2,1)S(1)} %copy.30), channel_id=1, source_target_pairs={{0,1},{1,2},{2,3},{3,4},{4,5},{5,6},{6,7},{7,0},{8,9},{9,10},{10,1... | collective-permute-start | bytes 393224 | tf_op jit(solution)/shard_map/while/body/eval_jaxpr/while/body/eval_jaxpr/ppermute | solution.py:50
  114.9 8.1 %collective-permute-start.3 = (bf16[128,8,64]{0,2,1:T(8,128)(2,1)S(1)}, bf16[128,8,64]{0,2,1:T(8,128)(2,1)S(1)}, u32[]{:S(2)}, u32[]{:S(2)}) collective-permute-start(bf16[128,8,64]{0,2,1:T(8,128)(2,1)S(1)} %copy.31), channel_id=1, source_target_pairs={{0,1},{1,2},{2,3},{3,4},{4,5},{5,6},{6,7},{7,0},{8,9},{9,10},{10,1... | collective-permute-start | bytes 393224 | tf_op jit(solution)/shard_map/while/body/eval_jaxpr/while/body/eval_jaxpr/ppermute | solution.py:51
  123.0 6.9 %collective-permute-start.2 = (bf16[128,8,64]{0,2,1:T(8,128)(2,1)S(1)}, bf16[128,8,64]{0,2,1:T(8,128)(2,1)S(1)}, u32[]{:S(2)}, u32[]{:S(2)}) collective-permute-start(bf16[128,8,64]{0,2,1:T(8,128)(2,1)S(1)} %copy.30), channel_id=1, source_target_pairs={{0,1},{1,2},{2,3},{3,4},{4,5},{5,6},{6,7},{7,0},{8,9},{9,10},{10,1... | collective-permute-start | bytes 393224 | tf_op jit(solution)/shard_map/while/body/eval_jaxpr/while/body/eval_jaxpr/ppermute | solution.py:50
  123.1 7.0 %collective-permute-start.3 = (bf16[128,8,64]{0,2,1:T(8,128)(2,1)S(1)}, bf16[128,8,64]{0,2,1:T(8,128)(2,1)S(1)}, u32[]{:S(2)}, u32[]{:S(2)}) collective-permute-start(bf16[128,8,64]{0,2,1:T(8,128)(2,1)S(1)} %copy.31), channel_id=1, source_target_pairs={{0,1},{1,2},{2,3},{3,4},{4,5},{5,6},{6,7},{7,0},{8,9},{9,10},{10,1... | collective-permute-start | bytes 393224 | tf_op jit(solution)/shard_map/while/body/eval_jaxpr/while/body/eval_jaxpr/ppermute | solution.py:51
  130.1 6.9 %collective-permute-start.2 = (bf16[128,8,64]{0,2,1:T(8,128)(2,1)S(1)}, bf16[128,8,64]{0,2,1:T(8,128)(2,1)S(1)}, u32[]{:S(2)}, u32[]{:S(2)}) collective-permute-start(bf16[128,8,64]{0,2,1:T(8,128)(2,1)S(1)} %copy.30), channel_id=1, source_target_pairs={{0,1},{1,2},{2,3},{3,4},{4,5},{5,6},{6,7},{7,0},{8,9},{9,10},{10,1... | collective-permute-start | bytes 393224 | tf_op jit(solution)/shard_map/while/body/eval_jaxpr/while/body/eval_jaxpr/ppermute | solution.py:50
  130.2 7.0 %collective-permute-start.3 = (bf16[128,8,64]{0,2,1:T(8,128)(2,1)S(1)}, bf16[128,8,64]{0,2,1:T(8,128)(2,1)S(1)}, u32[]{:S(2)}, u32[]{:S(2)}) collective-permute-start(bf16[128,8,64]{0,2,1:T(8,128)(2,1)S(1)} %copy.31), channel_id=1, source_target_pairs={{0,1},{1,2},{2,3},{3,4},{4,5},{5,6},{6,7},{7,0},{8,9},{9,10},{10,1... | collective-permute-start | bytes 393224 | tf_op jit(solution)/shard_map/while/body/eval_jaxpr/while/body/eval_jaxpr/ppermute | solution.py:51
  137.1 6.9 %collective-permute-start.2 = (bf16[128,8,64]{0,2,1:T(8,128)(2,1)S(1)}, bf16[128,8,64]{0,2,1:T(8,128)(2,1)S(1)}, u32[]{:S(2)}, u32[]{:S(2)}) collective-permute-start(bf16[128,8,64]{0,2,1:T(8,128)(2,1)S(1)} %copy.30), channel_id=1, source_target_pairs={{0,1},{1,2},{2,3},{3,4},{4,5},{5,6},{6,7},{7,0},{8,9},{9,10},{10,1... | collective-permute-start | bytes 393224 | tf_op jit(solution)/shard_map/while/body/eval_jaxpr/while/body/eval_jaxpr/ppermute | solution.py:50
  137.2 7.0 %collective-permute-start.3 = (bf16[128,8,64]{0,2,1:T(8,128)(2,1)S(1)}, bf16[128,8,64]{0,2,1:T(8,128)(2,1)S(1)}, u32[]{:S(2)}, u32[]{:S(2)}) collective-permute-start(bf16[128,8,64]{0,2,1:T(8,128)(2,1)S(1)} %copy.31), channel_id=1, source_target_pairs={{0,1},{1,2},{2,3},{3,4},{4,5},{5,6},{6,7},{7,0},{8,9},{9,10},{10,1... | collective-permute-start | bytes 393224 | tf_op jit(solution)/shard_map/while/body/eval_jaxpr/while/body/eval_jaxpr/ppermute | solution.py:51
  144.2 6.9 %collective-permute-start.2 = (bf16[128,8,64]{0,2,1:T(8,128)(2,1)S(1)}, bf16[128,8,64]{0,2,1:T(8,128)(2,1)S(1)}, u32[]{:S(2)}, u32[]{:S(2)}) collective-permute-start(bf16[128,8,64]{0,2,1:T(8,128)(2,1)S(1)} %copy.30), channel_id=1, source_target_pairs={{0,1},{1,2},{2,3},{3,4},{4,5},{5,6},{6,7},{7,0},{8,9},{9,10},{10,1... | collective-permute-start | bytes 393224 | tf_op jit(solution)/shard_map/while/body/eval_jaxpr/while/body/eval_jaxpr/ppermute | solution.py:50
  144.3 7.0 %collective-permute-start.3 = (bf16[128,8,64]{0,2,1:T(8,128)(2,1)S(1)}, bf16[128,8,64]{0,2,1:T(8,128)(2,1)S(1)}, u32[]{:S(2)}, u32[]{:S(2)}) collective-permute-start(bf16[128,8,64]{0,2,1:T(8,128)(2,1)S(1)} %copy.31), channel_id=1, source_target_pairs={{0,1},{1,2},{2,3},{3,4},{4,5},{5,6},{6,7},{7,0},{8,9},{9,10},{10,1... | collective-permute-start | bytes 393224 | tf_op jit(solution)/shard_map/while/body/eval_jaxpr/while/body/eval_jaxpr/ppermute | solution.py:51
  151.3 6.9 %collective-permute-start.2 = (bf16[128,8,64]{0,2,1:T(8,128)(2,1)S(1)}, bf16[128,8,64]{0,2,1:T(8,128)(2,1)S(1)}, u32[]{:S(2)}, u32[]{:S(2)}) collective-permute-start(bf16[128,8,64]{0,2,1:T(8,128)(2,1)S(1)} %copy.30), channel_id=1, source_target_pairs={{0,1},{1,2},{2,3},{3,4},{4,5},{5,6},{6,7},{7,0},{8,9},{9,10},{10,1... | collective-permute-start | bytes 393224 | tf_op jit(solution)/shard_map/while/body/eval_jaxpr/while/body/eval_jaxpr/ppermute | solution.py:50
  151.4 7.0 %collective-permute-start.3 = (bf16[128,8,64]{0,2,1:T(8,128)(2,1)S(1)}, bf16[128,8,64]{0,2,1:T(8,128)(2,1)S(1)}, u32[]{:S(2)}, u32[]{:S(2)}) collective-permute-start(bf16[128,8,64]{0,2,1:T(8,128)(2,1)S(1)} %copy.31), channel_id=1, source_target_pairs={{0,1},{1,2},{2,3},{3,4},{4,5},{5,6},{6,7},{7,0},{8,9},{9,10},{10,1... | collective-permute-start | bytes 393224 | tf_op jit(solution)/shard_map/while/body/eval_jaxpr/while/body/eval_jaxpr/ppermute | solution.py:51
  158.4 6.9 %collective-permute-start.2 = (bf16[128,8,64]{0,2,1:T(8,128)(2,1)S(1)}, bf16[128,8,64]{0,2,1:T(8,128)(2,1)S(1)}, u32[]{:S(2)}, u32[]{:S(2)}) collective-permute-start(bf16[128,8,64]{0,2,1:T(8,128)(2,1)S(1)} %copy.30), channel_id=1, source_target_pairs={{0,1},{1,2},{2,3},{3,4},{4,5},{5,6},{6,7},{7,0},{8,9},{9,10},{10,1... | collective-permute-start | bytes 393224 | tf_op jit(solution)/shard_map/while/body/eval_jaxpr/while/body/eval_jaxpr/ppermute | solution.py:50
  158.4 7.0 %collective-permute-start.3 = (bf16[128,8,64]{0,2,1:T(8,128)(2,1)S(1)}, bf16[128,8,64]{0,2,1:T(8,128)(2,1)S(1)}, u32[]{:S(2)}, u32[]{:S(2)}) collective-permute-start(bf16[128,8,64]{0,2,1:T(8,128)(2,1)S(1)} %copy.31), channel_id=1, source_target_pairs={{0,1},{1,2},{2,3},{3,4},{4,5},{5,6},{6,7},{7,0},{8,9},{9,10},{10,1... | collective-permute-start | bytes 393224 | tf_op jit(solution)/shard_map/while/body/eval_jaxpr/while/body/eval_jaxpr/ppermute | solution.py:51
  171.9 8.0 %collective-permute-start = (bf16[128,8,64]{0,2,1:T(8,128)(2,1)S(1)}, bf16[128,8,64]{0,2,1:T(8,128)(2,1)S(1)}, u32[]{:S(2)}, u32[]{:S(2)}) collective-permute-start(bf16[128,8,64]{0,2,1:T(8,128)(2,1)S(1)} %copy.66), channel_id=1, source_target_pairs={{0,1},{1,2},{2,3},{3,4},{4,5},{5,6},{6,7},{7,0},{8,9},{9,10},{10,1... | collective-permute-start | bytes 393224 | tf_op jit(solution)/shard_map/while/body/eval_jaxpr/ppermute | solution.py:50
  171.9 8.1 %collective-permute-start.1 = (bf16[128,8,64]{0,2,1:T(8,128)(2,1)S(1)}, bf16[128,8,64]{0,2,1:T(8,128)(2,1)S(1)}, u32[]{:S(2)}, u32[]{:S(2)}) collective-permute-start(bf16[128,8,64]{0,2,1:T(8,128)(2,1)S(1)} %copy.67), channel_id=1, source_target_pairs={{0,1},{1,2},{2,3},{3,4},{4,5},{5,6},{6,7},{7,0},{8,9},{9,10},{10,1... | collective-permute-start | bytes 393224 | tf_op jit(solution)/shard_map/while/body/eval_jaxpr/ppermute | solution.py:51
  180.1 6.9 %collective-permute-start = (bf16[128,8,64]{0,2,1:T(8,128)(2,1)S(1)}, bf16[128,8,64]{0,2,1:T(8,128)(2,1)S(1)}, u32[]{:S(2)}, u32[]{:S(2)}) collective-permute-start(bf16[128,8,64]{0,2,1:T(8,128)(2,1)S(1)} %copy.66), channel_id=1, source_target_pairs={{0,1},{1,2},{2,3},{3,4},{4,5},{5,6},{6,7},{7,0},{8,9},{9,10},{10,1... | collective-permute-start | bytes 393224 | tf_op jit(solution)/shard_map/while/body/eval_jaxpr/ppermute | solution.py:50
  180.2 7.0 %collective-permute-start.1 = (bf16[128,8,64]{0,2,1:T(8,128)(2,1)S(1)}, bf16[128,8,64]{0,2,1:T(8,128)(2,1)S(1)}, u32[]{:S(2)}, u32[]{:S(2)}) collective-permute-start(bf16[128,8,64]{0,2,1:T(8,128)(2,1)S(1)} %copy.67), channel_id=1, source_target_pairs={{0,1},{1,2},{2,3},{3,4},{4,5},{5,6},{6,7},{7,0},{8,9},{9,10},{10,1... | collective-permute-start | bytes 393224 | tf_op jit(solution)/shard_map/while/body/eval_jaxpr/ppermute | solution.py:51
  187.1 6.9 %collective-permute-start = (bf16[128,8,64]{0,2,1:T(8,128)(2,1)S(1)}, bf16[128,8,64]{0,2,1:T(8,128)(2,1)S(1)}, u32[]{:S(2)}, u32[]{:S(2)}) collective-permute-start(bf16[128,8,64]{0,2,1:T(8,128)(2,1)S(1)} %copy.66), channel_id=1, source_target_pairs={{0,1},{1,2},{2,3},{3,4},{4,5},{5,6},{6,7},{7,0},{8,9},{9,10},{10,1... | collective-permute-start | bytes 393224 | tf_op jit(solution)/shard_map/while/body/eval_jaxpr/ppermute | solution.py:50
  187.2 7.0 %collective-permute-start.1 = (bf16[128,8,64]{0,2,1:T(8,128)(2,1)S(1)}, bf16[128,8,64]{0,2,1:T(8,128)(2,1)S(1)}, u32[]{:S(2)}, u32[]{:S(2)}) collective-permute-start(bf16[128,8,64]{0,2,1:T(8,128)(2,1)S(1)} %copy.67), channel_id=1, source_target_pairs={{0,1},{1,2},{2,3},{3,4},{4,5},{5,6},{6,7},{7,0},{8,9},{9,10},{10,1... | collective-permute-start | bytes 393224 | tf_op jit(solution)/shard_map/while/body/eval_jaxpr/ppermute | solution.py:51
  194.2 6.9 %collective-permute-start = (bf16[128,8,64]{0,2,1:T(8,128)(2,1)S(1)}, bf16[128,8,64]{0,2,1:T(8,128)(2,1)S(1)}, u32[]{:S(2)}, u32[]{:S(2)}) collective-permute-start(bf16[128,8,64]{0,2,1:T(8,128)(2,1)S(1)} %copy.66), channel_id=1, source_target_pairs={{0,1},{1,2},{2,3},{3,4},{4,5},{5,6},{6,7},{7,0},{8,9},{9,10},{10,1... | collective-permute-start | bytes 393224 | tf_op jit(solution)/shard_map/while/body/eval_jaxpr/ppermute | solution.py:50
  194.3 7.0 %collective-permute-start.1 = (bf16[128,8,64]{0,2,1:T(8,128)(2,1)S(1)}, bf16[128,8,64]{0,2,1:T(8,128)(2,1)S(1)}, u32[]{:S(2)}, u32[]{:S(2)}) collective-permute-start(bf16[128,8,64]{0,2,1:T(8,128)(2,1)S(1)} %copy.67), channel_id=1, source_target_pairs={{0,1},{1,2},{2,3},{3,4},{4,5},{5,6},{6,7},{7,0},{8,9},{9,10},{10,1... | collective-permute-start | bytes 393224 | tf_op jit(solution)/shard_map/while/body/eval_jaxpr/ppermute | solution.py:51
  201.3 6.9 %collective-permute-start = (bf16[128,8,64]{0,2,1:T(8,128)(2,1)S(1)}, bf16[128,8,64]{0,2,1:T(8,128)(2,1)S(1)}, u32[]{:S(2)}, u32[]{:S(2)}) collective-permute-start(bf16[128,8,64]{0,2,1:T(8,128)(2,1)S(1)} %copy.66), channel_id=1, source_target_pairs={{0,1},{1,2},{2,3},{3,4},{4,5},{5,6},{6,7},{7,0},{8,9},{9,10},{10,1... | collective-permute-start | bytes 393224 | tf_op jit(solution)/shard_map/while/body/eval_jaxpr/ppermute | solution.py:50
  201.4 7.0 %collective-permute-start.1 = (bf16[128,8,64]{0,2,1:T(8,128)(2,1)S(1)}, bf16[128,8,64]{0,2,1:T(8,128)(2,1)S(1)}, u32[]{:S(2)}, u32[]{:S(2)}) collective-permute-start(bf16[128,8,64]{0,2,1:T(8,128)(2,1)S(1)} %copy.67), channel_id=1, source_target_pairs={{0,1},{1,2},{2,3},{3,4},{4,5},{5,6},{6,7},{7,0},{8,9},{9,10},{10,1... | collective-permute-start | bytes 393224 | tf_op jit(solution)/shard_map/while/body/eval_jaxpr/ppermute | solution.py:51
  208.3 6.9 %collective-permute-start = (bf16[128,8,64]{0,2,1:T(8,128)(2,1)S(1)}, bf16[128,8,64]{0,2,1:T(8,128)(2,1)S(1)}, u32[]{:S(2)}, u32[]{:S(2)}) collective-permute-start(bf16[128,8,64]{0,2,1:T(8,128)(2,1)S(1)} %copy.66), channel_id=1, source_target_pairs={{0,1},{1,2},{2,3},{3,4},{4,5},{5,6},{6,7},{7,0},{8,9},{9,10},{10,1... | collective-permute-start | bytes 393224 | tf_op jit(solution)/shard_map/while/body/eval_jaxpr/ppermute | solution.py:50
  208.4 7.0 %collective-permute-start.1 = (bf16[128,8,64]{0,2,1:T(8,128)(2,1)S(1)}, bf16[128,8,64]{0,2,1:T(8,128)(2,1)S(1)}, u32[]{:S(2)}, u32[]{:S(2)}) collective-permute-start(bf16[128,8,64]{0,2,1:T(8,128)(2,1)S(1)} %copy.67), channel_id=1, source_target_pairs={{0,1},{1,2},{2,3},{3,4},{4,5},{5,6},{6,7},{7,0},{8,9},{9,10},{10,1... | collective-permute-start | bytes 393224 | tf_op jit(solution)/shard_map/while/body/eval_jaxpr/ppermute | solution.py:51
  215.4 6.9 %collective-permute-start = (bf16[128,8,64]{0,2,1:T(8,128)(2,1)S(1)}, bf16[128,8,64]{0,2,1:T(8,128)(2,1)S(1)}, u32[]{:S(2)}, u32[]{:S(2)}) collective-permute-start(bf16[128,8,64]{0,2,1:T(8,128)(2,1)S(1)} %copy.66), channel_id=1, source_target_pairs={{0,1},{1,2},{2,3},{3,4},{4,5},{5,6},{6,7},{7,0},{8,9},{9,10},{10,1... | collective-permute-start | bytes 393224 | tf_op jit(solution)/shard_map/while/body/eval_jaxpr/ppermute | solution.py:50
  215.5 7.0 %collective-permute-start.1 = (bf16[128,8,64]{0,2,1:T(8,128)(2,1)S(1)}, bf16[128,8,64]{0,2,1:T(8,128)(2,1)S(1)}, u32[]{:S(2)}, u32[]{:S(2)}) collective-permute-start(bf16[128,8,64]{0,2,1:T(8,128)(2,1)S(1)} %copy.67), channel_id=1, source_target_pairs={{0,1},{1,2},{2,3},{3,4},{4,5},{5,6},{6,7},{7,0},{8,9},{9,10},{10,1... | collective-permute-start | bytes 393224 | tf_op jit(solution)/shard_map/while/body/eval_jaxpr/ppermute | solution.py:51
  (17 other events, 72.5 us)
where the time goes:
time: 230 us; the launch traced here: 226 us
  waiting for transfers between devices  134 us (58%)
  matrix products  48.8 us (21%)
  starting transfers between devices  21.8 us (9%)
  other arithmetic  14.3 us (6%)
  local copies, waits for them, and re-layouts  5.12 us (2%)
    ppermute x28, waiting for transfers between devices, step_x(): k_blk = lax.ppermute(k_blk, 'cx', perm_x)  116 us
    dot_general x32, matrix products, block_update(): jnp.einsum('qkgd,skd->kgqs', q_grouped, k_blk, preferred_element_type=jnp...  24.6 us
    dot_general x32, matrix products, block_update(): jnp.einsum('kgqs,skd->kgqd', prob_blk.astype(jnp.bfloat16), v_blk, prefer...  24.2 us
    ppermute x28, starting transfers between devices, step_x(): k_blk = lax.ppermute(k_blk, 'cx', perm_x)  15.1 us
    reduce_sum x32, other arithmetic, block_update(): row_sum = row_sum * rescale + jnp.sum(prob_blk, axis=-1)  13.3 us
    ppermute x28, waiting for transfers between devices, step_x(): v_blk = lax.ppermute(v_blk, 'cx', perm_x)  8.03 us
    ppermute x3, waiting for transfers between devices, step_y(): k_blk = lax.ppermute(k_blk, 'cy', perm_y)  6.78 us
  transfers between devices with their start and end apart: 62, of which 62 were waited for; matrix products, arithmetic and copies ran while one was open for 26% of the time, Pallas kernels for 0%

commit v1 on v0

v1 whole, which is shorter than its diff:
```python
import functools
import math

import jax
import jax.numpy as jnp
from jax import lax
from jax.experimental import pallas as pl
from jax.experimental.pallas import tpu as pltpu
from jax.sharding import PartitionSpec as P

F32 = jnp.float32
BF16 = jnp.bfloat16
MESH = pl.DeviceIdType.MESH

TILE = 256
MEMBERS = 8
BLOCKS = 4
EARLY = 2


def flip(value):
    return value + 1 - 2 * lax.rem(value, 2)


def attend_kernel(
    size_x, size_y, scale,
    q_ref, k_ref, v_ref, out_ref,
    q_got, kv_got, keys, q_limbs, scores, probs, block_max, row_max, row_sum, rescale, acc, out_send,
    kv_sent, kv_here, q_sent, q_here, fwd_sent, fwd_here, out_sent, out_here,
):
    head_dim, tokens = k_ref.shape[1:]
    group = q_ref.shape[0] // k_ref.shape[0]
    tiles = group * tokens // TILE
    per_tile = TILE // tokens
    span = MEMBERS * tokens
    steps = MEMBERS * BLOCKS
    turn = MEMBERS * EARLY
    late = BLOCKS - EARLY

    ix = lax.axis_index("cx")
    iy = lax.axis_index("cy")
    chips_x = size_x // 2
    chip_x, core = ix // 2, lax.rem(ix, 2)
    half_x, half_y = chips_x // 2, size_y // 2

    def head_of(x, y, c):
        px = lax.rem(x + x // half_x, 2)
        py = lax.rem(y + y // half_y, 2)
        return px * 4 + py * 2 + c

    def member(r):
        x = flip(chip_x) if r // 4 else chip_x
        y = flip(iy) if (r // 2) % 2 else iy
        c = flip(core) if r % 2 else core
        return {"cx": x * 2 + c, "cy": y}, head_of(x, y, c)

    my_head = head_of(chip_x, iy, core)
    mirror_x = {"cx": (chips_x - 1 - chip_x) * 2 + core, "cy": iy}
    mirror_y = {"cx": ix, "cy": size_y - 1 - iy}

    barrier = pltpu.get_barrier_semaphore()
    partners = [member(r)[0] for r in range(1, MEMBERS)] + [mirror_x, mirror_y]
    for who in partners:
        pl.semaphore_signal(barrier, inc=1, device_id=who, device_id_type=MESH)
    pl.semaphore_wait(barrier, len(partners))

    def remote(src, dst, sent, here, who):
        return pltpu.make_async_remote_copy(
            src_ref=src, dst_ref=dst, send_sem=sent, recv_sem=here, device_id=who, device_id_type=MESH
        )

    def send_kv(k_src, v_src, slot, sent, here, who):
        remote(k_src, slot.at[pl.ds(0, head_dim)], sent, here, who).start()
        remote(v_src, slot.at[pl.ds(head_dim, head_dim)], sent, here, who).start()

    def kv_whole(r):
        slot = kv_got.at[0, r]
        return remote(slot, slot, kv_sent.at[r], kv_here.at[r], member(r)[0])

    def q_copy(r):
        who, head = member(r)
        return remote(q_ref.at[pl.ds(head * group, group)], q_got.at[r], q_sent.at[r], q_here.at[r], who)

    def forward(block, r):
        index = (block - 1) * MEMBERS + r
        if block == 3:
            src, who = (kv_got.at[1, r], mirror_y) if r < 4 else (kv_got.at[2, r], mirror_x)
        else:
            src, who = kv_got.at[0, r], mirror_x if block == 1 else mirror_y
        return remote(src, kv_got.at[block, r], fwd_sent.at[index], fwd_here.at[index], who)

    def out_copy(r, head):
        return remote(
            out_send.at[r], out_ref.at[pl.ds(head * group, group)], out_sent.at[r], out_here.at[r], member(r)[0]
        )

    for r in range(1, MEMBERS):
        who, head = member(r)
        send_kv(k_ref.at[head], v_ref.at[head], kv_got.at[0, r], kv_sent.at[r], kv_here.at[r], who)
    for block, who in ((1, mirror_x), (2, mirror_y)):
        index = (block - 1) * MEMBERS
        send_kv(k_ref.at[my_head], v_ref.at[my_head], kv_got.at[block, 0], fwd_sent.at[index], fwd_here.at[index], who)
    for r in range(1, MEMBERS):
        q_copy(r).start()

    def prepare_keys(block, r, columns):
        base = block * span + r * tokens
        keys[pl.ds(base, tokens)] = jnp.transpose(jnp.concatenate([columns, columns], axis=0))

    def prepare_queries(r, read):
        for g in range(group):
            wide = read(g).astype(F32) * scale
            high = wide.astype(BF16)
            rest = wide - high.astype(F32)
            middle = rest.astype(BF16)
            low = (rest - middle.astype(F32)).astype(BF16)
            cols = pl.ds(g % per_tile * tokens, tokens)
            for n, term in enumerate((high, middle, low)):
                q_limbs[r, g // per_tile, pl.ds(n * head_dim, head_dim), cols] = term

    def step_q(i):
        return jnp.where(i < turn, lax.rem(i, MEMBERS), MEMBERS - 1 - (i - turn) // late)

    def step_b(i):
        return jnp.where(i < turn, i // MEMBERS, EARLY + lax.rem(i, late))

    def score(i):
        r, b = step_q(i), step_b(i)
        doubled = keys[pl.ds(pl.multiple_of(b * span, span), span)]
        lhs = jnp.concatenate([doubled, doubled], axis=1)
        for t in range(tiles):
            s = jnp.dot(lhs, q_limbs[r, t], preferred_element_type=F32)
            scores[t] = s
            block_max[t] = jnp.max(s.reshape(span // 8, 8, TILE), axis=0)

    def soften(i):
        r = step_q(i)
        for t in range(tiles):
            old = row_max[r, t]
            new = jnp.maximum(old, jnp.max(block_max[t], axis=0, keepdims=True))
            row_max[r, t] = new
            factor = jnp.exp2(old - new)
            rescale[t] = factor
            p = jnp.exp2(scores[t].reshape(span // 8, 8, TILE) - new[None])
            row_sum[r, t] = row_sum[r, t] * factor + jnp.sum(p, axis=0)
            probs[t] = p.reshape(span, TILE).astype(BF16)

    def weigh(i):
        r, b = step_q(i), step_b(i)
        values = jnp.concatenate([kv_got[b, m, pl.ds(head_dim, head_dim)] for m in range(MEMBERS)], axis=1)
        for t in range(tiles):
            weighted = jnp.dot(values, probs[t], preferred_element_type=F32)
            acc[r, t] = acc[r, t] * rescale[t][0:1] + weighted

    def body(i, carry=0):
        weigh(jnp.maximum(i - 1, 0))
        soften(i)
        score(i + 1)
        return carry

    def run(start, stop):
        if stop > start:
            lax.fori_loop(start, stop, body, 0)

    def finish(r):
        for t in range(tiles):
            inverse = 1.0 / jnp.sum(row_sum[r, t], axis=0, keepdims=True)
            result = (acc[r, t] * inverse).astype(BF16)
            for n in range(per_tile):
                part = result[:, n * tokens:(n + 1) * tokens]
                if r == 0:
                    out_ref[my_head * group + t * per_tile + n] = part
                else:
                    out_send[r, t * per_tile + n] = part

    row_max[...] = jnp.full_like(row_max, -jnp.inf)
    row_sum[...] = jnp.zeros_like(row_sum)
    rescale[...] = jnp.ones_like(rescale)
    acc[...] = jnp.zeros_like(acc)
    probs[...] = jnp.zeros_like(probs)
    q_limbs[:, :, pl.ds(3 * head_dim, TILE - 3 * head_dim)] = jnp.zeros(
        (MEMBERS, tiles, TILE - 3 * head_dim, TILE), BF16
    )
    prepare_queries(0, lambda g: q_ref[my_head * group + g])
    prepare_keys(0, 0, k_ref[my_head])
    kv_got[0, 0, pl.ds(head_dim, head_dim)] = v_ref[my_head]

    for r in range(1, MEMBERS):
        kv_whole(r).wait_recv()
        forward(1, r).start()
        forward(2, r).start()
        prepare_keys(0, r, kv_got[0, r, :head_dim])
    score(0)
    for r in range(1, MEMBERS):
        q_copy(r).wait_recv()
        prepare_queries(r, lambda g: q_got[r, g])
        if r == 3:
            for m in range(4):
                forward(1, m).wait_recv()
                forward(3, m).start()
        if r == 6:
            for m in range(4, MEMBERS):
                forward(2, m).wait_recv()
                forward(3, m).start()
        run(r - 1, r)

    done = MEMBERS - 1
    for block in range(1, BLOCKS):
        first = block * MEMBERS if block <= EARLY else turn + block - EARLY
        run(done, first - 1)
        done = first - 1
        for r in range(MEMBERS):
            if (block, r // 4) not in ((1, 0), (2, 1)):
                forward(block, r).wait_recv()
        for r in range(MEMBERS):
            prepare_keys(block, r, kv_got[block, r, :head_dim])

    for r in range(MEMBERS - 1, 0, -1):
        stop = turn + (MEMBERS - r) * late + 1
        if stop < steps:
            run(done, stop)
            done = stop
        else:
            run(done, steps - 1)
            done = steps - 1
        if r < MEMBERS - 1:
            out_copy(r + 1, my_head).start()
        finish(r)
    assert done == steps - 1
    weigh(steps - 2)
    soften(steps - 1)
    out_copy(1, my_head).start()
    weigh(steps - 1)
    finish(0)

    for r in range(1, MEMBERS):
        out_copy(r, member(r)[1]).wait_recv()
        out_copy(r, my_head).wait_send()
        kv_whole(r).wait_send()
        q_copy(r).wait_send()
    for block in range(1, BLOCKS):
        for r in range(MEMBERS):
            forward(block, r).wait_send()


def solution(mesh):
    size_x = mesh.shape["cx"]
    size_y = mesh.shape["cy"]
    seq_spec = P(("batch", "cx", "cy"), None, None)

    def local_attention(q_local, k_local, v_local):
        tokens, num_heads, head_dim = q_local.shape
        num_kv = k_local.shape[1]
        group = num_heads // num_kv
        tiles = group * tokens // TILE
        span = MEMBERS * tokens
        scale = 1.0 / math.sqrt(head_dim) / math.log(2.0)
        vmem = pl.BlockSpec(memory_space=pltpu.VMEM)
        out_cols = pl.pallas_call(
            functools.partial(attend_kernel, size_x, size_y, scale),
            out_shape=jax.ShapeDtypeStruct((num_heads, head_dim, tokens), BF16),
            in_specs=[vmem] * 3,
            out_specs=vmem,
            scratch_shapes=[
                pltpu.VMEM((MEMBERS, group, head_dim, tokens), BF16),
                pltpu.VMEM((BLOCKS, MEMBERS, 2 * head_dim, tokens), BF16),
                pltpu.VMEM((BLOCKS * span, 2 * head_dim), BF16),
                pltpu.VMEM((MEMBERS, tiles, TILE, TILE), BF16),
                pltpu.VMEM((tiles, span, TILE), F32),
                pltpu.VMEM((tiles, span, TILE), BF16),
                pltpu.VMEM((tiles, 8, TILE), F32),
                pltpu.VMEM((MEMBERS, tiles, 8, TILE), F32),
                pltpu.VMEM((MEMBERS, tiles, 8, TILE), F32),
                pltpu.VMEM((tiles, 8, TILE), F32),
                pltpu.VMEM((MEMBERS, tiles, head_dim, TILE), F32),
                pltpu.VMEM((MEMBERS, group, head_dim, tokens), BF16),
                pltpu.SemaphoreType.DMA((MEMBERS,)),
                pltpu.SemaphoreType.DMA((MEMBERS,)),
                pltpu.SemaphoreType.DMA((MEMBERS,)),
                pltpu.SemaphoreType.DMA((MEMBERS,)),
                pltpu.SemaphoreType.DMA(((BLOCKS - 1) * MEMBERS,)),
                pltpu.SemaphoreType.DMA(((BLOCKS - 1) * MEMBERS,)),
                pltpu.SemaphoreType.DMA((MEMBERS,)),
                pltpu.SemaphoreType.DMA((MEMBERS,)),
            ],
            compiler_params=pltpu.CompilerParams(collective_id=0, has_side_effects=True),
        )(*(jnp.transpose(x, (1, 2, 0)) for x in (q_local, k_local, v_local)))
        return jnp.transpose(out_cols, (2, 0, 1))

    return jax.shard_map(
        local_attention, mesh=mesh, in_specs=(seq_spec, seq_spec, seq_spec), out_specs=seq_spec, check_vma=False
    )
```

time: 230 us -> 41.9 us (0.18); the launches traced: 226 us -> 41.8 us
  waiting for transfers between devices: 134 us -> 0 us
  matrix products: 48.8 us -> 0 us
  Pallas kernels: 0 us -> 39.9 us
  starting transfers between devices: 21.8 us -> 0 us
  other arithmetic: 14.3 us -> 0 us
  local copies, waits for them, and re-layouts: 5.12 us -> 1.87 us
    ppermute x62 -> x0, waiting for transfers between devices: 134 us -> none  [the longest x28 116 us: step_x(): k_blk = lax.ppermute(k_blk, 'cx', perm_x)]
    dot_general x64 -> x0, matrix products: 48.8 us -> none  [the longest x32 24.6 us: block_update(): jnp.einsum('qkgd,skd->kgqs', q_grouped, k_blk, preferred_element_type=jnp...]
    pallas_call x0 -> x1, Pallas kernels: none -> 39.9 us  [local_attention(): pl.pallas_call(functools.partial(attend_kernel, size_x, size_y, scale), o...]
    ppermute x62 -> x0, starting transfers between devices: 21.8 us -> none  [the longest x28 15.1 us: step_x(): k_blk = lax.ppermute(k_blk, 'cx', perm_x)]
    reduce_sum x32 -> x0, other arithmetic: 13.3 us -> none  [block_update(): row_sum = row_sum * rescale + jnp.sum(prob_blk, axis=-1)]
    while x40 -> x0, local copies, waits for them, and re-layouts: 2.76 us -> none
  transfers between devices with their start and end apart: 62 -> 0, of which waited for: 62 -> 0; matrix products, arithmetic and copies ran while one was open for 26% -> 0% of each run, Pallas kernels for 0% -> 0%
where the time goes in v1:
time: 41.9 us; the launch traced here: 41.8 us
  Pallas kernels  39.9 us (95%)
  local copies, waits for them, and re-layouts  1.87 us (4%)
    pallas_call x1, Pallas kernels, local_attention(): pl.pallas_call(functools.partial(attend_kernel, size_x, size_y, scale), o...  39.9 us
    unnamed x1, local copies, waits for them, and re-layouts  1.87 us

profile of v1, /device:TPU:97, one launch (start us, length us, event | category | flops | bytes accessed | tf_op | source)
XLA Modules:
  0.0 41.8 jit_solution(1397520011049295571)
XLA Ops:
  0.0 39.9 %shard_map.37 = bf16[32,64,128]{2,1,0:T(8,128)(2,1)} custom-call(bf16[32,64,128]{2,1,0:T(8,128)(2,1)} %bitcast.5, bf16[8,64,128]{2,1,0:T(8,128)(2,1)} %bitcast.6, bf16[8,64,128]{2,1,0:T(8,128)(2,1)} %bitcast.7), custom_call_target="tpu_custom_call" | custom-call | tf_op jit(solution)/shard_map/pallas_call | solution.py:259
  39.9 1.9 %copy.5 = bf16[128,32,64]{0,2,1:T(8,128)(2,1)} copy(bf16[128,32,64]{0,2,1:T(8,128)(2,1)} %bitcast.4) | data formatting | bytes 1048576
